TPU v7x, 256 devices: a whole 4x4x8 slice. The times are simulated.
256 devices in a mesh: outer: 8 (over x, y_hi), inner: 32 (over y_lo, z, core).
Axes of the slice: x: 4, y: 4 (y_hi: 2, y_lo: 2; y = y_hi * 2 + y_lo), z: 8, core: 2. Of those that a mesh axis runs over, the one named last changes fastest.
Arguments:
- tokens: bfloat16 [32768, 4096], P('inner', 'outer'), may hold values from -6 to 6
- cotangent: bfloat16 [32768, 4096], P('inner', 'outer'), may hold values from -0.03125 to 0.03125
- weight_cache: bfloat16 [4096, 4096], P(None, 'outer'), may hold values from -0.09375 to 0.09375
- weight_delta: bfloat16 [4096, 4096], P('inner', 'outer'), may hold values from -0.078125 to 0.078125
- sign_bits: int32 [4096], P('outer'), may hold values from 0 to 1
- master: float32 [4096, 4096], P('inner', 'outer'), may hold values from -1.5 to 1.5
- moment: float32 [4096, 4096], P('inner', 'outer'), may hold values from -6 to 6
- variance: float32 [4096, 4096], P('inner', 'outer'), may hold values from 0.25 to 4
Outputs:
- activation: float32 [32768, 4096], P('inner', 'outer')
- new_master: float32 [4096, 4096], P('inner', 'outer')
- new_moment: float32 [4096, 4096], P('inner', 'outer')
- new_variance: float32 [4096, 4096], P('inner', 'outer')
- block_scales: float32 [4096, 32], P('inner', 'outer')
All inputs are finite; a program needn't handle non-finite values.
Results may differ from a plain program's by a relative error of at most 0.003.
Values may be sent and summed in bfloat16 or wider, within the bound.
A program may use at most 128 MiB of HBM per device.

v0:
```python
import jax
import jax.numpy as jnp
from jax import lax
from jax.sharding import Mesh
from jax.sharding import PartitionSpec as P

BLOCK = 128
INNER = ("inner_0", "inner_1", "inner_2")


def split_up(value, dim, devices):
    before, after = (value.shape[:dim], value.shape[dim + 1 :])
    return jnp.moveaxis(value.reshape(*before, devices, -1, *after), dim, 0)


def summed_rows(value, chips, core, dim):
    sizes = (lax.axis_size(chips), lax.axis_size(core))
    blocks = split_up(value, dim, sizes[0] * sizes[1])
    inside = blocks.shape[1:]
    blocks = blocks.reshape(*sizes, *inside).swapaxes(0, 1).reshape(-1, *inside)
    blocks = lax.psum_scatter(blocks, core, scatter_dimension=0, tiled=True)
    return lax.psum_scatter(blocks, chips, scatter_dimension=0, tiled=True)[0]


def hadamard_table(length):
    first = jnp.arange(length, dtype=jnp.int32)[:, None]
    second = jnp.arange(length, dtype=jnp.int32)[None, :]
    common = jnp.bitwise_and(first, second)
    parity = jnp.zeros((length, length), jnp.int32)
    for place in range(length.bit_length() - 1):
        parity = parity + jnp.bitwise_and(jnp.right_shift(common, place), 1)
    return (1 - 2 * (parity % 2)).astype(jnp.float32) / jnp.sqrt(jnp.float32(length))


def smooth(values, signs, table):
    height = values.shape[0]
    blocks = values.reshape(height, -1, table.shape[0]) * signs.reshape(-1, table.shape[0])
    mixed = jnp.einsum("rbk,kj->rbj", blocks, table, precision=lax.Precision.HIGHEST)
    return mixed.reshape(height, -1)


def unsmooth(values, signs, table):
    height = values.shape[0]
    blocks = values.reshape(height, -1, table.shape[0])
    mixed = jnp.einsum("rbj,jk->rbk", blocks, table, precision=lax.Precision.HIGHEST)
    return (mixed * signs.reshape(-1, table.shape[0])).reshape(height, -1)


def outer_product(left, right):
    return lax.dot_general(
        left, right, (((0,), (0,)), ((), ())), preferred_element_type=jnp.float32
    )


def body(tokens, cotangent, weight_cache, weight_delta, sign_bits, master, moment, variance):
    table = hadamard_table(BLOCK)
    signs = (1 - 2 * sign_bits).astype(jnp.float32)
    shard_rows = master.shape[0]
    gathered = lax.all_gather(tokens, "outer", axis=1, tiled=True)
    merged = (
        weight_cache.astype(jnp.float32)
        + lax.all_gather(weight_delta, INNER, axis=0, tiled=True).astype(jnp.float32)
    ).astype(jnp.bfloat16)
    columns = gathered
    output = jnp.dot(columns, merged, preferred_element_type=jnp.float32)
    columns = gathered
    partial_value = outer_product(columns, cotangent)
    summed = summed_rows(partial_value, ("inner_0", "inner_1"), "inner_2", 0)
    smoothed = smooth(summed, signs, table)
    block_scales = jnp.max(jnp.abs(smoothed.reshape(shard_rows, -1, BLOCK)), axis=2)
    restored = unsmooth(smoothed, signs, table)
    new_moment = 0.9 * moment + 0.1 * restored
    new_variance = 0.95 * variance + 0.05 * restored * restored
    corrected = new_moment / (1.0 - 0.9**10)
    spread = jnp.sqrt(new_variance / (1.0 - 0.95**10)) + 1e-08
    new_master = master - 0.01 * (corrected / spread + 0.1 * master)
    return (output, new_master, new_moment, new_variance, block_scales)


def solution(mesh):
    torus = Mesh(
        mesh.devices.reshape(mesh.shape["outer"], 2, 8, 2),
        ("outer", "inner_0", "inner_1", "inner_2"),
    )
    in_specs = (
        P(INNER, "outer"),
        P(INNER, "outer"),
        P(None, "outer"),
        P(INNER, "outer"),
        P("outer"),
        P(INNER, "outer"),
        P(INNER, "outer"),
        P(INNER, "outer"),
    )
    out_specs = (
        P(INNER, "outer"),
        P(INNER, "outer"),
        P(INNER, "outer"),
        P(INNER, "outer"),
        P(INNER, "outer"),
    )
    return jax.shard_map(body, mesh=torus, in_specs=in_specs, out_specs=out_specs, check_vma=False)
```

profile of v0, /device:TPU:6, one launch (start us, length us, event | category | flops | bytes accessed | tf_op | source)
XLA Modules:
  0.0 268.3 jit_solution(17581240308026730228)
XLA Ops:
  8.0 0.0 copy-start
  8.0 0.0 all-gather.5.cloned.1.call-start
  8.1 0.7 all-gather.5.cloned.1.call-update
  8.7 0.0 reduce-scatter.3.cloned.1.call-start
  8.8 129.7 %all-gather.5.cloned.1.call-done = bf16[1024,4096]{1,0:T(8,128)(2,1)} async-done(((bf16[1024,512]{1,0:T(8,128)(2,1)}), bf16[1024,4096]{1,0:T(8,128)(2,1)}) %all-gather.5.cloned.1.call-update) | async-done | bytes 8388624 | tf_op jit(solution)/shard_map/all_gather | solution.py:59
  138.5 0.0 copy-done
  138.5 7.1 %fusion.47 = f32[4096,512]{1,0:T(8,128)S(1)} fusion(bf16[1024,4096]{1,0:T(8,128)(2,1)} %all-gather.5.cloned.1.call-done, bf16[1024,512]{1,0:T(8,128)(2,1)S(1)} %copy-done), kind=kOutput, calls=%fused_computation.54 | convolution fusion | flops 4294967296 | bytes 17825792 | tf_op jit(solution)/shard_map/dot_general | solution.py:50
  145.6 4.2 %copy.19 = f32[16,2,128,512]{3,2,0,1:T(8,128)} copy(f32[16,2,128,512]{3,2,1,0:T(8,128)S(1)} %bitcast.21) | data formatting | bytes 16777216 | tf_op jit(solution)/shard_map/reshape;reshape | solution.py:20
  149.9 0.0 reduce-scatter.3.cloned.1.call-update
  149.9 0.0 all-gather.3.cloned.1.call-start
  150.0 0.5 all-gather.3.cloned.1.call-update
  150.5 0.0 reduce-scatter.5.cloned.1.call-start
  150.6 20.5 %reduce-scatter.3.cloned.1.call-done = f32[16,128,512]{2,1,0:T(8,128)} async-done(((f32[32,128,512]{2,1,0:T(8,128)}), f32[16,128,512]{2,1,0:T(8,128)}) %reduce-scatter.3.cloned.1.call-update) | async-done | bytes 4194320 | tf_op jit(solution)/shard_map/reduce_scatter | solution.py:21
  171.0 0.0 reduce-scatter.5.cloned.1.call-update
  171.1 0.0 copy-start.1
  171.1 57.4 %all-gather.3.cloned.1.call-done = bf16[4096,512]{1,0:T(8,128)(2,1)} async-done(((bf16[128,512]{1,0:T(8,128)(2,1)}), bf16[4096,512]{1,0:T(8,128)(2,1)}) %all-gather.3.cloned.1.call-update) | async-done | bytes 4194320 | tf_op jit(solution)/shard_map/all_gather | solution.py:62
  228.5 9.6 %fusion.1 = f32[1024,512]{0,1:T(8,128)S(1)} fusion(bf16[1024,4096]{1,0:T(8,128)(2,1)} %all-gather.5.cloned.1.call-done, bf16[4096,512]{1,0:T(8,128)(2,1)} %all-gather.3.cloned.1.call-done, bf16[4096,512]{1,0:T(8,128)(2,1)} %param.10), kind=kOutput, calls=%fused_computation.2 | convolution fusion | flops 4303355904 | bytes 18874368 | tf_op jit(solution)/shard_map/dot_general | solution.py:65
  238.0 1.8 copy.26
  239.9 16.5 %reduce-scatter.5.cloned.1.call-done = f32[1,128,512]{2,1,0:T(8,128)} async-done(((f32[16,128,512]{2,1,0:T(8,128)}), f32[1,128,512]{2,1,0:T(8,128)}) %reduce-scatter.5.cloned.1.call-update) | async-done | bytes 262160 | tf_op jit(solution)/shard_map/reduce_scatter | solution.py:22
  256.4 1.1 copy.20
  257.5 1.1 abs_reduce_fusion
  258.6 0.4 convolution_multiply_fusion
  259.0 0.1 copy.23
  259.2 2.0 multiply_subtract_fusion
  (4 shorter events, 0.0 us)
Async XLA Ops:
  8.0 130.5 %copy-start = (bf16[1024,512]{1,0:T(8,128)(2,1)S(1)}, bf16[1024,512]{1,0:T(8,128)(2,1)}, u32[]{:S(2)}) copy-start(bf16[1024,512]{1,0:T(8,128)(2,1)} %param.9) | copy-start | bytes 3145732
  8.0 130.5 %all-gather.5.cloned.1.call-start = ((), (), s32[]{:S(2)}) async-start(), calls=%async_computation.3 | async-start | bytes 9437184 | tf_op jit(solution)/shard_map/all_gather | solution.py:59
  8.7 162.3 %reduce-scatter.3.cloned.1.call-start = ((), (), s32[]{:S(2)}) async-start(), calls=%async_computation.4 | async-start | bytes 12582912 | tf_op jit(solution)/shard_map/reduce_scatter | solution.py:21
  149.9 21.2 %copy-start.2 = (s32[512]{0:T(512)S(1)}, s32[512]{0:T(512)}, u32[]{:S(2)}) copy-start(s32[512]{0:T(512)} %param.12) | copy-start | bytes 6148
  149.9 78.5 %all-gather.3.cloned.1.call-start = ((), (), s32[]{:S(2)}) async-start(), calls=%async_computation.2 | async-start | bytes 4325376 | tf_op jit(solution)/shard_map/all_gather | solution.py:62
  150.5 105.9 %reduce-scatter.5.cloned.1.call-start = ((), (), s32[]{:S(2)}) async-start(), calls=%async_computation.5 | async-start | bytes 4456448 | tf_op jit(solution)/shard_map/reduce_scatter | solution.py:22
  171.1 88.1 %copy-start.1 = (f32[128,512]{1,0:T(8,128)S(1)}, f32[128,512]{1,0:T(8,128)}, u32[]{:S(2)}) copy-start(f32[128,512]{1,0:T(8,128)} %param.13) | copy-start | bytes 786436
Sparse Core Ops, SparseCore 0:
  11.3 127.1 all-gather.4
  150.0 20.9 reduce-scatter.2
  173.6 82.7 reduce-scatter.4
Sparse Core Ops, SparseCore 1:
  152.3 76.1 all-gather.2
where the time goes:
time: 268 us
  waiting for transfers between devices  225 us (84%)
  matrix products  18.3 us (7%)
  between operations  15.3 us (6%)
  local copies, waits for them, and re-layouts  7.28 us (3%)
    all_gather x1, waiting for transfers between devices, body(): gathered = lax.all_gather(tokens, 'outer', axis=1, tiled=True)  130 us
    all_gather x1, waiting for transfers between devices, body(): lax.all_gather(weight_delta, INNER, axis=0, tiled=True).astype(jnp.float32)  57.4 us
    reduce_scatter x1, waiting for transfers between devices, summed_rows(): blocks = lax.psum_scatter(blocks, core, scatter_dimension=0, tiled=True)  20.5 us
    reduce_scatter x1, waiting for transfers between devices, summed_rows(): return lax.psum_scatter(blocks, chips, scatter_dimension=0, tiled=True)[0]  16.5 us
    dot_general x1, matrix products, body(): output = jnp.dot(columns, merged, preferred_element_type=jnp.float32)  9.58 us
    dot_general x1, matrix products, outer_product(): lax.dot_general(left, right, (((0,), (0,)), ((), ())), preferred_element_...  7.13 us
  transfers between devices with their start and end apart: 4, of which 4 were waited for; matrix products, arithmetic and copies ran while one was open for 4% of the time, Pallas kernels for 0%

commit v1 on v0

--- a/solution.py
+++ b/solution.py
@@ -59,7 +59,9 @@
     gathered = lax.all_gather(tokens, "outer", axis=1, tiled=True)
     merged = (
         weight_cache.astype(jnp.float32)
-        + lax.all_gather(weight_delta, INNER, axis=0, tiled=True).astype(jnp.float32)
+        + jnp.concatenate(
+            lax.all_to_all(jnp.stack([weight_delta] * lax.axis_size(INNER)), INNER, 0, 0), axis=0
+        ).astype(jnp.float32)
     ).astype(jnp.bfloat16)
     columns = gathered
     output = jnp.dot(columns, merged, preferred_element_type=jnp.float32)

time: 268 us -> 316 us (1.18)
  waiting for transfers between devices: 225 us -> 263 us
  starting transfers between devices: 0.16 us -> 7.67 us
  local copies, waits for them, and re-layouts: 7.28 us -> 10.6 us
    all_to_all x0 -> x1, waiting for transfers between devices: none -> 114 us  [body(): lax.all_to_all(jnp.stack([weight_delta] * lax.axis_size(INNER)), INNER, 0...]
    all_gather x1 -> x0, waiting for transfers between devices: 57.4 us -> none  [body(): lax.all_gather(weight_delta, INNER, axis=0, tiled=True).astype(jnp.float32)]
    reduce_scatter x1, waiting for transfers between devices: 20.5 us -> 10.2 us  [summed_rows(): blocks = lax.psum_scatter(blocks, core, scatter_dimension=0, tiled=True)]
    reduce_scatter x1, waiting for transfers between devices: 16.5 us -> 8.3 us  [summed_rows(): return lax.psum_scatter(blocks, chips, scatter_dimension=0, tiled=True)[0]]
    all_to_all x0 -> x1, starting transfers between devices: none -> 7.55 us  [body(): lax.all_to_all(jnp.stack([weight_delta] * lax.axis_size(INNER)), INNER, 0...]
where the time goes in v1:
time: 316 us
  waiting for transfers between devices  263 us (83%)
  matrix products  18.2 us (6%)
  between operations  13.8 us (4%)
  local copies, waits for them, and re-layouts  10.6 us (3%)
  starting transfers between devices  7.67 us (2%)
    all_gather x1, waiting for transfers between devices, body(): gathered = lax.all_gather(tokens, 'outer', axis=1, tiled=True)  130 us
    all_to_all x1, waiting for transfers between devices, body(): lax.all_to_all(jnp.stack([weight_delta] * lax.axis_size(INNER)), INNER, 0...  114 us
    reduce_scatter x1, waiting for transfers between devices, summed_rows(): blocks = lax.psum_scatter(blocks, core, scatter_dimension=0, tiled=True)  10.2 us
    dot_general x1, matrix products, body(): output = jnp.dot(columns, merged, preferred_element_type=jnp.float32)  9.57 us
    reduce_scatter x1, waiting for transfers between devices, summed_rows(): return lax.psum_scatter(blocks, chips, scatter_dimension=0, tiled=True)[0]  8.3 us
    all_to_all x1, starting transfers between devices, body(): lax.all_to_all(jnp.stack([weight_delta] * lax.axis_size(INNER)), INNER, 0...  7.55 us
    dot_general x1, matrix products, outer_product(): lax.dot_general(left, right, (((0,), (0,)), ((), ())), preferred_element_...  7.13 us
  transfers between devices with their start and end apart: 4, of which 4 were waited for; matrix products, arithmetic and copies ran while one was open for 4% of the time, Pallas kernels for 0%

profile of v1, /device:TPU:6, one launch (start us, length us, event | category | flops | bytes accessed | tf_op | source)
XLA Modules:
  0.0 315.6 jit_solution(1942898206413471297)
XLA Ops:
  7.2 0.0 copy-start
  7.2 0.0 all-gather.2.cloned.1.call-start
  7.2 0.7 all-gather.2.cloned.1.call-update
  7.9 0.0 reduce-scatter.3.cloned.1.call-start
  8.0 129.7 %all-gather.2.cloned.1.call-done = bf16[1024,4096]{1,0:T(8,128)(2,1)} async-done(((bf16[1024,512]{1,0:T(8,128)(2,1)}), bf16[1024,4096]{1,0:T(8,128)(2,1)}) %all-gather.2.cloned.1.call-update) | async-done | bytes 8388624 | tf_op jit(solution)/shard_map/all_gather | solution.py:59
  137.7 0.0 copy-done
  137.7 7.1 %fusion.51 = f32[4096,512]{1,0:T(8,128)S(1)} fusion(bf16[1024,4096]{1,0:T(8,128)(2,1)} %all-gather.2.cloned.1.call-done, bf16[1024,512]{1,0:T(8,128)(2,1)S(1)} %copy-done), kind=kOutput, calls=%fused_computation.55 | convolution fusion | flops 4294967296 | bytes 17825792 | tf_op jit(solution)/shard_map/dot_general | solution.py:50
  144.8 4.2 %copy.19 = f32[16,2,128,512]{3,2,0,1:T(8,128)} copy(f32[16,2,128,512]{3,2,1,0:T(8,128)S(1)} %bitcast.23) | data formatting | bytes 16777216 | tf_op jit(solution)/shard_map/reshape;reshape | solution.py:20
  149.1 0.0 reduce-scatter.3.cloned.1.call-update
  149.1 0.9 copy-done.2
  150.0 2.4 stack.2
  152.4 7.6 %all-to-all-start = ((bf16[32,128,512]{2,1,0:T(8,128)(2,1)}), bf16[32,128,512]{2,1,0:T(8,128)(2,1)}, u32[]{:S(2)}, u32[]{:S(2)}) async-start(bf16[32,128,512]{2,1,0:T(8,128)(2,1)} %stack.2), calls=%async_computation | async-start | bytes 8388608 | tf_op jit(solution)/shard_map/all_to_all | solution.py:63
  160.0 0.0 reduce-scatter.5.cloned.1.call-start
  160.0 10.2 %reduce-scatter.3.cloned.1.call-done = f32[16,128,512]{2,1,0:T(8,128)} async-done(((f32[32,128,512]{2,1,0:T(8,128)}), f32[16,128,512]{2,1,0:T(8,128)}) %reduce-scatter.3.cloned.1.call-update) | async-done | bytes 4194320 | tf_op jit(solution)/shard_map/reduce_scatter | solution.py:21
  170.2 0.0 reduce-scatter.5.cloned.1.call-update
  170.3 114.3 %all-to-all-done = bf16[32,128,512]{2,1,0:T(8,128)(2,1)} async-done(((bf16[32,128,512]{2,1,0:T(8,128)(2,1)}), bf16[32,128,512]{2,1,0:T(8,128)(2,1)}, u32[]{:S(2)}, u32[]{:S(2)}) %all-to-all-start) | async-done | bytes 4194336 | tf_op jit(solution)/shard_map/all_to_all | solution.py:63
  284.6 9.6 %fusion.3 = f32[1024,512]{0,1:T(8,128)S(1)} fusion(bf16[1024,4096]{1,0:T(8,128)(2,1)} %all-gather.2.cloned.1.call-done, bf16[4096,512]{1,0:T(8,128)(2,1)} %bitcast.9, bf16[4096,512]{1,0:T(8,128)(2,1)} %param.10), kind=kOutput, calls=%fused_computation.3 | convolution fusion | flops 4303355904 | bytes 18874368 | tf_op jit(solution)/shard_map/dot_general | solution.py:67
  294.2 1.8 copy.26
  296.0 8.3 %reduce-scatter.5.cloned.1.call-done = f32[1,128,512]{2,1,0:T(8,128)} async-done(((f32[16,128,512]{2,1,0:T(8,128)}), f32[1,128,512]{2,1,0:T(8,128)}) %reduce-scatter.5.cloned.1.call-update) | async-done | bytes 262160 | tf_op jit(solution)/shard_map/reduce_scatter | solution.py:22
  304.3 1.1 copy.20
  305.4 1.1 abs_reduce_fusion
  306.5 0.4 convolution_multiply_fusion
  306.9 0.1 copy.23
  307.1 2.0 multiply_subtract_fusion
  (6 shorter events, 0.0 us)
Async XLA Ops:
  7.2 130.5 %copy-start = (bf16[1024,512]{1,0:T(8,128)(2,1)S(1)}, bf16[1024,512]{1,0:T(8,128)(2,1)}, u32[]{:S(2)}) copy-start(bf16[1024,512]{1,0:T(8,128)(2,1)} %param.9) | copy-start | bytes 3145732
  7.2 130.5 %all-gather.2.cloned.1.call-start = ((), (), s32[]{:S(2)}) async-start(), calls=%async_computation.3 | async-start | bytes 9437184 | tf_op jit(solution)/shard_map/all_gather | solution.py:59
  7.9 162.3 %reduce-scatter.3.cloned.1.call-start = ((), (), s32[]{:S(2)}) async-start(), calls=%async_computation.4 | async-start | bytes 12582912 | tf_op jit(solution)/shard_map/reduce_scatter | solution.py:21
  149.1 0.9 copy-start.2
  150.0 20.3 %copy-start.3 = (s32[512]{0:T(512)S(1)}, s32[512]{0:T(512)}, u32[]{:S(2)}) copy-start(s32[512]{0:T(512)} %param.12) | copy-start | bytes 6148
  152.4 132.2 %all-to-all-start = ((bf16[32,128,512]{2,1,0:T(8,128)(2,1)}), bf16[32,128,512]{2,1,0:T(8,128)(2,1)}, u32[]{:S(2)}, u32[]{:S(2)}) async-start(bf16[32,128,512]{2,1,0:T(8,128)(2,1)} %stack.2), calls=%async_computation | async-start | bytes 8388608 | tf_op jit(solution)/shard_map/all_to_all | solution.py:63
  160.0 144.3 %reduce-scatter.5.cloned.1.call-start = ((), (), s32[]{:S(2)}) async-start(), calls=%async_computation.5 | async-start | bytes 4456448 | tf_op jit(solution)/shard_map/reduce_scatter | solution.py:22
  284.6 22.5 %copy-start.1 = (f32[128,512]{1,0:T(8,128)S(1)}, f32[128,512]{1,0:T(8,128)}, u32[]{:S(2)}) copy-start(f32[128,512]{1,0:T(8,128)} %param.13) | copy-start | bytes 786436
Sparse Core Ops, SparseCore 0:
  10.5 127.1 all-gather.1
  149.2 20.9 reduce-scatter.2
  172.8 131.4 reduce-scatter.4
